TPU v7x, 32 devices: a whole 2x2x4 slice. The times are simulated.
32 devices in a mesh: view: 4 (over x, core), gz: 8 (over z, y).
Axes of the slice: x: 2, y: 2, z: 4, core: 2. Of those that a mesh axis runs over, the one named last changes fastest.
Arguments:
- views_data: float32 [4, 128, 128, 384], P('view', 'gz'), may hold values from 0.25 to 4
- start: float32 [128, 128, 384], P('gz'), may hold values from 0.5 to 2
- psf_table: float32 [8, 3, 17], replicated, may hold values from 0.05 to 1
- psf_index: int32 [4], P('view'), may hold values from 0 to 7
Outputs:
- estimate: float32 [128, 128, 384], P('gz')
All inputs are finite; a program needn't handle non-finite values.
Results may differ from a plain program's by a relative error of at most 0.0001.
Values sent between devices are 32-bit elements; how exact they have to be, the bound alone decides.
A program may use at most 128 MiB of HBM per device.

v0:
```python
import jax
import jax.numpy as jnp
from jax import lax
from jax.sharding import PartitionSpec as P

ITERS = 2


def with_halo(block, sides, width):
    for axis, dim in sides:
        count = lax.axis_size(axis)
        forward = [(i, i + 1) for i in range(count - 1)]
        backward = [(target, source) for source, target in forward]
        low = lax.ppermute(
            lax.slice_in_dim(block, block.shape[dim] - width, None, axis=dim), axis, forward
        )
        high = lax.ppermute(lax.slice_in_dim(block, 0, width, axis=dim), axis, backward)
        block = jnp.concatenate([low, block, high], axis=dim)
    return block


def band_matrix(kern_row, length, radius):
    places = jnp.arange(length)
    offsets = places[None, :] - places[:, None]
    tap_shift = jnp.arange(2 * radius + 1) - radius
    matches = (offsets[None, :, :] == tap_shift[:, None, None]).astype(jnp.float32)
    return jnp.sum(kern_row[:, None, None] * matches, axis=0)


def blur_planes(volume, mat_x, mat_y):
    along_x = jnp.einsum("ij,zjy->ziy", mat_x, volume, precision=lax.Precision.HIGHEST)
    return jnp.einsum("zxj,ij->zxi", along_x, mat_y, precision=lax.Precision.HIGHEST)


def back_planes(volume, mat_x, mat_y):
    along_x = jnp.einsum("ij,ziy->zjy", mat_x, volume, precision=lax.Precision.HIGHEST)
    return jnp.einsum("zxi,ij->zxj", along_x, mat_y, precision=lax.Precision.HIGHEST)


def forward_z(padded, kern_z, rows, radius):
    total = kern_z[0] * padded[0:rows]
    for tap in range(1, 2 * radius + 1):
        total = total + kern_z[tap] * padded[tap : tap + rows]
    return total


def backward_z(padded, kern_z, rows, radius):
    total = kern_z[0] * padded[2 * radius : 2 * radius + rows]
    for tap in range(1, 2 * radius + 1):
        total = total + kern_z[tap] * padded[2 * radius - tap : 2 * radius - tap + rows]
    return total


def on_device(views_data, start, psf_table, psf_index):
    slab = views_data[0]
    planes_dev, width_x, width_y = start.shape
    radius = (psf_table.shape[2] - 1) // 2
    sections = lax.axis_size("view")
    picked = (jnp.arange(psf_table.shape[0]) == psf_index[0]).astype(jnp.float32)
    kern = jnp.sum(picked[:, None, None] * psf_table, axis=0)
    kern = kern / jnp.sum(kern, axis=-1, keepdims=True)
    mat_x = band_matrix(kern[1], width_x, radius)
    mat_y = band_matrix(kern[2], width_y, radius)
    estimate = start
    for step in range(ITERS):
        planes = blur_planes(estimate, mat_x, mat_y)
        widened = with_halo(planes, (("gz", 0),), radius)
        blurred = forward_z(widened, kern[0], planes_dev, radius)
        ratio = slab / blurred
        ratio_wide = with_halo(ratio, (("gz", 0),), radius)
        smeared = backward_z(ratio_wide, kern[0], planes_dev, radius)
        correction = back_planes(smeared, mat_x, mat_y)
        share = width_x // sections
        received = lax.all_to_all(correction[None], "view", split_axis=2, concat_axis=0, tiled=True)
        total = received[0]
        for member in range(1, sections):
            total = total * received[member]
        own_part = lax.dynamic_slice_in_dim(estimate, lax.axis_index("view") * share, share, 1)
        updated = own_part * jnp.power(total, 1.0 / sections)
        estimate = lax.all_gather(updated, "view", axis=1, tiled=True)
    return estimate


def solution(mesh):
    return jax.shard_map(
        on_device,
        mesh=mesh,
        in_specs=(P("view", "gz", None, None), P("gz", None, None), P(), P("view")),
        out_specs=P("gz", None, None),
        check_vma=False,
    )
```

profile of v0, /device:TPU:0, one launch (start us, length us, event | category | flops | bytes accessed | tf_op | source)
XLA Modules:
  0.0 616.6 jit_solution(12783196030434788462)
XLA Ops:
  7.3 0.9 multiply_reduce_fusion
  8.1 0.1 broadcast_divide_fusion
  8.2 0.2 select_reduce_fusion.1
  8.4 1.0 select_reduce_fusion
  9.5 4.6 fusion.288
  14.1 6.0 fusion.230
  20.1 0.0 copy-start.2
  20.1 0.3 fusion.295
  20.4 5.1 collective-permute-start
  25.5 1.5 collective-permute-start.1
  27.1 0.7 fusion.296
  27.8 65.0 %collective-permute-done = f32[8,128,384]{2,1,0:T(8,128)S(1)} collective-permute-done((f32[8,128,384]{2,1,0:T(8,128)S(1)}, f32[8,128,384]{2,1,0:T(8,128)S(1)}, u32[]{:S(2)}, u32[]{:S(2)}) %collective-permute-start) | collective-permute-done | bytes 1572896 | tf_op jit(solution)/shard_map/ppermute | solution.py:14
  92.8 0.0 collective-permute-done.1
  92.8 0.0 copy-start.4
  92.8 1.1 copy-done.4
  93.9 0.0 copy-done.2
  93.9 19.2 %fusion.167 = f32[16,128,384]{2,1,0:T(8,128)S(1)} fusion(f32[16,128,384]{2,1,0:T(8,128)S(1)} %fusion.230, f32[8,128,384]{2,1,0:T(8,128)} %copy-done.4, f32[8,128,384]{2,1,0:T(8,128)S(1)} %collective-permute-done, f32[1,16,128,384]{3,2,1,0:T(8,128)S(1)} %copy-done.2, f32[]{:T(128)} %bitcast.23, f32[]{:T(128)} %bitcast.22, f32[]{:T(128)} %bitcast.21, ...), kind=kLoop, calls=%fused_computation.252 | loop fusion | flops 39321600 | bytes 12582980 | tf_op jit(solution)/shard_map/div | solution.py:69
  113.1 0.0 copy-start.1
  113.2 1.7 copy-done.1
  114.8 0.3 fusion.294
  115.1 1.3 collective-permute-start.2
  116.4 6.2 %collective-permute-start.3 = (f32[8,128,384]{2,1,0:T(8,128)S(1)}, f32[8,128,384]{2,1,0:T(8,128)}, u32[]{:S(2)}, u32[]{:S(2)}) collective-permute-start(f32[8,128,384]{2,1,0:T(8,128)S(1)} %get-tuple-element.12), channel_id=1, source_target_pairs={{0,1},{1,2},{2,3},{3,4},{4,5},{5,6},{6,7},{8,9},{9,10},{10,11},{11... | collective-permute-start | bytes 4718600 | tf_op jit(solution)/shard_map/ppermute | solution.py:14
  122.6 30.4 %collective-permute-done.2 = f32[8,128,384]{2,1,0:T(8,128)S(1)} collective-permute-done((f32[8,128,384]{2,1,0:T(8,128)S(1)}, f32[8,128,384]{2,1,0:T(8,128)S(1)}, u32[]{:S(2)}, u32[]{:S(2)}) %collective-permute-start.2) | collective-permute-done | bytes 1572896 | tf_op jit(solution)/shard_map/ppermute | solution.py:17
  153.0 34.7 %collective-permute-done.3 = f32[8,128,384]{2,1,0:T(8,128)} collective-permute-done((f32[8,128,384]{2,1,0:T(8,128)S(1)}, f32[8,128,384]{2,1,0:T(8,128)}, u32[]{:S(2)}, u32[]{:S(2)}) %collective-permute-start.3) | collective-permute-done | bytes 1572896 | tf_op jit(solution)/shard_map/ppermute | solution.py:14
  187.7 32.9 %fusion.108 = f32[16,384,128]{2,1,0:T(8,128)} fusion(f32[16,128,384]{2,1,0:T(8,128)} %copy-done.1, f32[8,128,384]{2,1,0:T(8,128)} %collective-permute-done.3, f32[8,128,384]{2,1,0:T(8,128)S(1)} %collective-permute-done.2, f32[]{:T(128)} %bitcast.23, f32[]{:T(128)} %bitcast.22, f32[]{:T(128)} %bitcast.21, f32[]{:T(128)} %bitcast.20, f32[]{:T(128)} %bitcast.19, ...), kind=kOutput, calls=%fused_computation.207 | convolution fusion | flops 1246494720 | bytes 9502788 | tf_op jit(solution)/shard_map/ij,ziy->zjy/dot_general | solution.py:36
  220.6 8.4 %fusion.234 = f32[1,16,128,384]{3,2,1,0:T(8,128)S(1)} fusion(f32[16,384,128]{2,1,0:T(8,128)} %fusion.108, f32[384,384]{1,0:T(8,128)S(1)} %select_reduce_fusion), kind=kOutput, calls=%fused_computation.325 | convolution fusion | flops 3623878656 | bytes 6881280 | tf_op jit(solution)/shard_map/zxi,ij->zxj/dot_general | solution.py:37
  229.0 3.5 copy.20
  232.5 4.7 all-to-all-start
  237.2 0.0 all-gather.3.cloned.1.call-start
  237.2 36.9 %all-to-all-done = f32[1,16,128,384]{3,1,0,2:T(8,128)} async-done(((f32[1,16,128,384]{3,1,0,2:T(8,128)}), f32[1,16,128,384]{3,1,0,2:T(8,128)}, u32[]{:S(2)}, u32[]{:S(2)}) %all-to-all-start) | async-done | bytes 3145760 | tf_op jit(solution)/shard_map/all_to_all | solution.py:74
  274.1 2.9 copy.41
  277.0 2.4 fusion.279
  279.4 0.0 all-gather.3.cloned.1.call-update
  279.4 8.8 %all-gather.5.cloned.1.call-start = ((), (), s32[]{:S(2)}) async-start(), calls=%async_computation.3 | async-start | bytes 3932160 | tf_op jit(solution)/shard_map/all_gather | solution.py:80
  288.2 20.4 %all-gather.3.cloned.1.call-done = f32[16,128,384]{2,1,0:T(8,128)} async-done(((f32[16,32,384]{2,1,0:T(8,128)}), f32[16,128,384]{2,1,0:T(8,128)}) %all-gather.3.cloned.1.call-update) | async-done | bytes 3145744 | tf_op jit(solution)/shard_map/all_gather | solution.py:80
  308.6 6.9 %fusion.285 = f32[16,384,128]{2,1,0:T(8,128)S(1)} fusion(f32[16,128,384]{2,1,0:T(8,128)} %all-gather.3.cloned.1.call-done, f32[128,128]{1,0:T(8,128)S(1)} %select_reduce_fusion.1), kind=kOutput, calls=%fused_computation.380 | convolution fusion | flops 1207959552 | bytes 6356992 | tf_op jit(solution)/shard_map/ij,zjy->ziy/dot_general | solution.py:31
  315.6 10.2 %fusion.226 = f32[16,128,384]{2,1,0:T(8,128)S(1)} fusion(f32[16,384,128]{2,1,0:T(8,128)S(1)} %fusion.285, f32[384,384]{1,0:T(8,128)S(1)} %select_reduce_fusion), kind=kOutput, calls=%fused_computation.316 | convolution fusion | flops 3623878656 | bytes 6881280 | tf_op jit(solution)/shard_map/zxj,ij->zxi/dot_general | solution.py:32
  325.8 0.0 copy-start.3
  325.8 0.3 fusion.293
  326.1 3.6 collective-permute-start.4
  329.7 1.3 collective-permute-start.5
  331.0 66.3 %collective-permute-done.4 = f32[8,128,384]{2,1,0:T(8,128)S(1)} collective-permute-done((f32[8,128,384]{2,1,0:T(8,128)S(1)}, f32[8,128,384]{2,1,0:T(8,128)S(1)}, u32[]{:S(2)}, u32[]{:S(2)}) %collective-permute-start.4) | collective-permute-done | bytes 1572896 | tf_op jit(solution)/shard_map/ppermute | solution.py:14
  397.3 0.0 collective-permute-done.5
  397.4 0.0 copy-done.3
  397.4 19.1 %fusion.63 = f32[16,128,384]{2,1,0:T(8,128)S(1)} fusion(f32[16,128,384]{2,1,0:T(8,128)S(1)} %fusion.226, f32[8,128,384]{2,1,0:T(8,128)} %collective-permute-done.5, f32[8,128,384]{2,1,0:T(8,128)S(1)} %collective-permute-done.4, f32[1,16,128,384]{3,2,1,0:T(8,128)S(1)} %copy-done.3, f32[]{:T(128)} %bitcast.23, f32[]{:T(128)} %bitcast.22, f32[]{:T(128)} %bitcast.21, ...), kind=kLoop, calls=%fused_computation.162 | loop fusion | flops 39321600 | bytes 12582980 | tf_op jit(solution)/shard_map/div | solution.py:69
  416.5 0.0 copy-start
  416.5 1.7 copy-done
  418.2 0.3 fusion.292
  418.5 1.3 collective-permute-start.6
  419.8 6.2 %collective-permute-start.7 = (f32[8,128,384]{2,1,0:T(8,128)S(1)}, f32[8,128,384]{2,1,0:T(8,128)}, u32[]{:S(2)}, u32[]{:S(2)}) collective-permute-start(f32[8,128,384]{2,1,0:T(8,128)S(1)} %get-tuple-element.8), channel_id=1, source_target_pairs={{0,1},{1,2},{2,3},{3,4},{4,5},{5,6},{6,7},{8,9},{9,10},{10,11},{11... | collective-permute-start | bytes 4718600 | tf_op jit(solution)/shard_map/ppermute | solution.py:14
  425.9 30.8 %collective-permute-done.6 = f32[8,128,384]{2,1,0:T(8,128)S(1)} collective-permute-done((f32[8,128,384]{2,1,0:T(8,128)S(1)}, f32[8,128,384]{2,1,0:T(8,128)S(1)}, u32[]{:S(2)}, u32[]{:S(2)}) %collective-permute-start.6) | collective-permute-done | bytes 1572896 | tf_op jit(solution)/shard_map/ppermute | solution.py:17
  456.8 34.3 %collective-permute-done.7 = f32[8,128,384]{2,1,0:T(8,128)} collective-permute-done((f32[8,128,384]{2,1,0:T(8,128)S(1)}, f32[8,128,384]{2,1,0:T(8,128)}, u32[]{:S(2)}, u32[]{:S(2)}) %collective-permute-start.7) | collective-permute-done | bytes 1572896 | tf_op jit(solution)/shard_map/ppermute | solution.py:14
  491.1 32.4 %fusion.4 = f32[16,384,128]{2,1,0:T(8,128)} fusion(f32[16,128,384]{2,1,0:T(8,128)} %copy-done, f32[8,128,384]{2,1,0:T(8,128)} %collective-permute-done.7, f32[8,128,384]{2,1,0:T(8,128)S(1)} %collective-permute-done.6, f32[]{:T(128)} %bitcast.23, f32[]{:T(128)} %bitcast.22, f32[]{:T(128)} %bitcast.21, f32[]{:T(128)} %bitcast.20, f32[]{:T(128)} %bitcast.19, ...), kind=kOutput, calls=%fused_computation.117 | convolution fusion | flops 1246494720 | bytes 9502788 | tf_op jit(solution)/shard_map/ij,ziy->zjy/dot_general | solution.py:36
  523.5 8.4 %fusion.237 = f32[1,16,128,384]{3,2,1,0:T(8,128)S(1)} fusion(f32[16,384,128]{2,1,0:T(8,128)} %fusion.4, f32[384,384]{1,0:T(8,128)S(1)} %select_reduce_fusion), kind=kOutput, calls=%fused_computation.326 | convolution fusion | flops 3623878656 | bytes 6881280 | tf_op jit(solution)/shard_map/zxi,ij->zxj/dot_general | solution.py:37
  531.9 1.8 copy.26
  533.7 39.4 %all_to_all.30 = f32[1,16,128,384]{3,1,0,2:T(8,128)S(1)} all-to-all(f32[1,16,128,384]{3,1,0,2:T(8,128)S(1)} %copy.26), channel_id=1, replica_groups=mesh['view'=4,'gz'=8] {'view'}, dimensions={2} | all-to-all | bytes 6291456 | tf_op jit(solution)/shard_map/all_to_all | solution.py:74
  573.1 1.0 copy.40
  574.1 2.4 fusion.276
  576.5 0.0 all-gather.5.cloned.1.call-update
  576.5 29.0 %all-gather.5.cloned.1.call-done = f32[16,128,384]{2,1,0:T(8,128)} async-done(((f32[16,32,384]{2,1,0:T(8,128)}), f32[16,128,384]{2,1,0:T(8,128)}) %all-gather.5.cloned.1.call-update) | async-done | bytes 3145744 | tf_op jit(solution)/shard_map/all_gather | solution.py:80
  605.6 3.9 copy.44
  (5 shorter events, 0.1 us)
Async XLA Ops:
  20.1 73.8 %copy-start.2 = (f32[1,16,128,384]{3,2,1,0:T(8,128)S(1)}, f32[1,16,128,384]{3,2,1,0:T(8,128)}, u32[]{:S(2)}) copy-start(f32[1,16,128,384]{3,2,1,0:T(8,128)} %param.4) | copy-start | bytes 9437188
  20.4 72.4 %collective-permute-start = (f32[8,128,384]{2,1,0:T(8,128)S(1)}, f32[8,128,384]{2,1,0:T(8,128)S(1)}, u32[]{:S(2)}, u32[]{:S(2)}) collective-permute-start(f32[8,128,384]{2,1,0:T(8,128)S(1)} %get-tuple-element.13), channel_id=1, source_target_pairs={{0,1},{1,2},{2,3},{3,4},{4,5},{5,6},{6,7},{8,9},{9,10},{10,11},{11... | collective-permute-start | bytes 4718600 | tf_op jit(solution)/shard_map/ppermute | solution.py:14
  25.5 67.2 %collective-permute-start.1 = (f32[8,128,384]{2,1,0:T(8,128)S(1)}, f32[8,128,384]{2,1,0:T(8,128)S(1)}, u32[]{:S(2)}, u32[]{:S(2)}) collective-permute-start(f32[8,128,384]{2,1,0:T(8,128)S(1)} %get-tuple-element.14), channel_id=1, source_target_pairs={{1,0},{2,1},{3,2},{4,3},{5,4},{6,5},{7,6},{9,8},{10,9},{11,10},{12... | collective-permute-start | bytes 4718600 | tf_op jit(solution)/shard_map/ppermute | solution.py:17
  92.8 1.1 copy-start.4
  113.1 1.7 copy-start.1
  115.1 37.9 %collective-permute-start.2 = (f32[8,128,384]{2,1,0:T(8,128)S(1)}, f32[8,128,384]{2,1,0:T(8,128)S(1)}, u32[]{:S(2)}, u32[]{:S(2)}) collective-permute-start(f32[8,128,384]{2,1,0:T(8,128)S(1)} %get-tuple-element.11), channel_id=1, source_target_pairs={{1,0},{2,1},{3,2},{4,3},{5,4},{6,5},{7,6},{9,8},{10,9},{11,10},{12... | collective-permute-start | bytes 4718600 | tf_op jit(solution)/shard_map/ppermute | solution.py:17
  116.4 71.3 %collective-permute-start.3 = (f32[8,128,384]{2,1,0:T(8,128)S(1)}, f32[8,128,384]{2,1,0:T(8,128)}, u32[]{:S(2)}, u32[]{:S(2)}) collective-permute-start(f32[8,128,384]{2,1,0:T(8,128)S(1)} %get-tuple-element.12), channel_id=1, source_target_pairs={{0,1},{1,2},{2,3},{3,4},{4,5},{5,6},{6,7},{8,9},{9,10},{10,11},{11... | collective-permute-start | bytes 4718600 | tf_op jit(solution)/shard_map/ppermute | solution.py:14
  232.5 41.6 %all-to-all-start = ((f32[1,16,128,384]{3,1,0,2:T(8,128)}), f32[1,16,128,384]{3,1,0,2:T(8,128)}, u32[]{:S(2)}, u32[]{:S(2)}) async-start(f32[1,16,128,384]{3,1,0,2:T(8,128)} %copy.20), calls=%async_computation | async-start | bytes 6291456 | tf_op jit(solution)/shard_map/all_to_all | solution.py:74
  237.2 71.5 %all-gather.3.cloned.1.call-start = ((), (), s32[]{:S(2)}) async-start(), calls=%async_computation.2 | async-start | bytes 3932160 | tf_op jit(solution)/shard_map/all_gather | solution.py:80
  279.4 326.2 %all-gather.5.cloned.1.call-start = ((), (), s32[]{:S(2)}) async-start(), calls=%async_computation.3 | async-start | bytes 3932160 | tf_op jit(solution)/shard_map/all_gather | solution.py:80
  325.8 71.6 %copy-start.3 = (f32[1,16,128,384]{3,2,1,0:T(8,128)S(1)}, f32[1,16,128,384]{3,2,1,0:T(8,128)}, u32[]{:S(2)}) copy-start(f32[1,16,128,384]{3,2,1,0:T(8,128)} %param.4) | copy-start | bytes 9437188
  326.1 71.3 %collective-permute-start.4 = (f32[8,128,384]{2,1,0:T(8,128)S(1)}, f32[8,128,384]{2,1,0:T(8,128)S(1)}, u32[]{:S(2)}, u32[]{:S(2)}) collective-permute-start(f32[8,128,384]{2,1,0:T(8,128)S(1)} %get-tuple-element.9), channel_id=1, source_target_pairs={{0,1},{1,2},{2,3},{3,4},{4,5},{5,6},{6,7},{8,9},{9,10},{10,11},{11... | collective-permute-start | bytes 4718600 | tf_op jit(solution)/shard_map/ppermute | solution.py:14
  329.7 67.6 %collective-permute-start.5 = (f32[8,128,384]{2,1,0:T(8,128)S(1)}, f32[8,128,384]{2,1,0:T(8,128)}, u32[]{:S(2)}, u32[]{:S(2)}) collective-permute-start(f32[8,128,384]{2,1,0:T(8,128)S(1)} %get-tuple-element.10), channel_id=1, source_target_pairs={{1,0},{2,1},{3,2},{4,3},{5,4},{6,5},{7,6},{9,8},{10,9},{11,10},{12... | collective-permute-start | bytes 4718600 | tf_op jit(solution)/shard_map/ppermute | solution.py:17
  416.5 1.7 copy-start
  418.5 38.3 %collective-permute-start.6 = (f32[8,128,384]{2,1,0:T(8,128)S(1)}, f32[8,128,384]{2,1,0:T(8,128)S(1)}, u32[]{:S(2)}, u32[]{:S(2)}) collective-permute-start(f32[8,128,384]{2,1,0:T(8,128)S(1)} %get-tuple-element.7), channel_id=1, source_target_pairs={{1,0},{2,1},{3,2},{4,3},{5,4},{6,5},{7,6},{9,8},{10,9},{11,10},{12... | collective-permute-start | bytes 4718600 | tf_op jit(solution)/shard_map/ppermute | solution.py:17
  419.8 71.4 %collective-permute-start.7 = (f32[8,128,384]{2,1,0:T(8,128)S(1)}, f32[8,128,384]{2,1,0:T(8,128)}, u32[]{:S(2)}, u32[]{:S(2)}) collective-permute-start(f32[8,128,384]{2,1,0:T(8,128)S(1)} %get-tuple-element.8), channel_id=1, source_target_pairs={{0,1},{1,2},{2,3},{3,4},{4,5},{5,6},{6,7},{8,9},{9,10},{10,11},{11... | collective-permute-start | bytes 4718600 | tf_op jit(solution)/shard_map/ppermute | solution.py:14
Sparse Core Ops, SparseCore 0:
  279.5 29.0 all-gather.2
  576.7 28.8 all-gather.4
where the time goes:
time: 626 us; the launch traced here: 617 us
  waiting for transfers between devices  348 us (56%)
  matrix products  110 us (18%)
  other arithmetic  45.4 us (7%)
  starting transfers between devices  40 us (6%)
  blocking collectives  39.4 us (6%)
  local copies, waits for them, and re-layouts  19.3 us (3%)
  between operations  14.7 us (2%)
    ppermute x4, waiting for transfers between devices, with_halo(): lax.ppermute(lax.slice_in_dim(block, block.shape[dim] - width, None, axis...  200 us
    dot_general x2, matrix products, back_planes(): jnp.einsum('ij,ziy->zjy', mat_x, volume, precision=lax.Precision.HIGHEST)  65.3 us
    ppermute x4, waiting for transfers between devices, with_halo(): lax.ppermute(lax.slice_in_dim(block, 0, width, axis=dim), axis, backward)  61.3 us
    all_gather x2, waiting for transfers between devices, on_device(): estimate = lax.all_gather(updated, 'view', axis=1, tiled=True)  49.4 us
    all_to_all x1, blocking collectives, on_device(): lax.all_to_all(correction[None], 'view', split_axis=2, concat_axis=0, til...  39.4 us
    div x2, other arithmetic, on_device(): ratio = slab / blurred  38.4 us
    all_to_all x1, waiting for transfers between devices, on_device(): lax.all_to_all(correction[None], 'view', split_axis=2, concat_axis=0, til...  36.9 us
    ppermute x4, starting transfers between devices, with_halo(): lax.ppermute(lax.slice_in_dim(block, block.shape[dim] - width, None, axis...  21.1 us
  transfers between devices with their start and end apart: 11, of which 9 were waited for; matrix products, arithmetic and copies ran while one was open for 0% of the time, Pallas kernels for 0%

commit v1 on v0

v1 whole, which is shorter than its diff:
```python
import functools
import jax
import jax.numpy as jnp
from jax import lax
from jax.experimental import pallas as pl
from jax.experimental.pallas import tpu as pltpu
from jax.sharding import PartitionSpec as P

ITERS = 2
AXES = ("view", "gz")
GROUP = 4
VMEM = pl.BlockSpec(memory_space=pltpu.VMEM)
SMEM = pl.BlockSpec(memory_space=pltpu.SMEM)
PARAMS = pltpu.CompilerParams(vmem_limit_bytes=40 * 1024 * 1024)


def split(value):
    high = value.astype(jnp.bfloat16)
    return high, (value - high.astype(jnp.float32)).astype(jnp.bfloat16)


def dot3(lhs, rhs):
    (lh, ll), (rh, rl) = lhs, rhs
    dot = functools.partial(jnp.dot, preferred_element_type=jnp.float32)
    return dot(lh, rh) + (dot(ll, rh) + dot(lh, rl))


def taps_sum(kz_ref, source, flip):
    taps = kz_ref.shape[0]
    total = kz_ref[taps - 1 if flip else 0] * source(0)
    for tap in range(1, taps):
        total = total + kz_ref[taps - 1 - tap if flip else tap] * source(tap)
    return total


def forward_kernel(kz_ref, e_ref, d_ref, ax_ref, my_ref, r_ref, zc_ref):
    rows_in, width = e_ref.shape[1], e_ref.shape[2]
    rows = d_ref.shape[1]
    ax = split(ax_ref[...])
    my = split(my_ref[...])

    @pl.loop(0, d_ref.shape[0] // GROUP)
    def _(step):
        base = step * GROUP
        for plane in range(GROUP):
            for tile in range(rows_in // 8):
                at = pl.ds(tile * 8, 8)
                zc_ref[pl.ds(plane * rows_in + tile * 8, 8), :] = taps_sum(
                    kz_ref, lambda tap: e_ref[base + plane + tap, at, :], False
                )
        along_x = dot3(ax, split(zc_ref[...]))
        blurred = dot3(split(along_x), my)
        r_ref[pl.ds(base, GROUP)] = d_ref[pl.ds(base, GROUP)] / blurred.reshape(GROUP, rows, width)


def smear_kernel(kz_ref, low_ref, r_ref, high_ref, u_ref):
    planes, pad = r_ref.shape[0], low_ref.shape[0]

    def source(place):
        if place < pad:
            return low_ref[place]
        if place < pad + planes:
            return r_ref[place - pad]
        return high_ref[place - pad - planes]

    for plane in range(planes):
        u_ref[plane] = taps_sum(kz_ref, lambda tap: source(plane + tap), True)


def back_kernel(low_ref, u_ref, high_ref, ax_ref, my_ref, *rest):
    out_ref, wide_ref = rest[-2:]
    rows, width = u_ref.shape[1], u_ref.shape[2]
    pad = low_ref.shape[1]
    wide = rows + 2 * pad
    ax = split(ax_ref[...])
    my = split(my_ref[...])

    @pl.loop(0, u_ref.shape[0] // GROUP)
    def _(step):
        base = step * GROUP
        for plane in range(GROUP):
            wide_ref[pl.ds(plane * wide, pad), :] = low_ref[base + plane]
            wide_ref[pl.ds(plane * wide + pad, rows), :] = u_ref[base + plane]
            wide_ref[pl.ds(plane * wide + pad + rows, pad), :] = high_ref[base + plane]
        along_x = dot3(ax, split(wide_ref[...]))
        result = dot3(split(along_x), my).reshape(GROUP, rows, width)
        if len(rest) == 3:
            result = result * rest[0][pl.ds(base, GROUP)]
        out_ref[pl.ds(base, GROUP)] = result


def blur_forward(kz, wide, data, ax, my):
    planes, rows, width = data.shape
    return pl.pallas_call(
        forward_kernel,
        out_shape=jax.ShapeDtypeStruct(data.shape, jnp.float32),
        in_specs=[SMEM, VMEM, VMEM, VMEM, VMEM],
        out_specs=VMEM,
        scratch_shapes=[pltpu.VMEM((GROUP * wide.shape[1], width), jnp.float32)],
        compiler_params=PARAMS,
        cost_estimate=pl.CostEstimate(
            flops=data.size * 2 * width * 12, bytes_accessed=16 * data.size, transcendentals=0
        ),
    )(kz, wide, data, ax, my)


def smear(kz, low, ratio, high):
    planes, rows, width = ratio.shape
    pad = low.shape[0]
    block = lambda depth: pl.BlockSpec((depth, 8, width), lambda i: (0, i, 0))
    return pl.pallas_call(
        smear_kernel,
        grid=(rows // 8,),
        out_shape=jax.ShapeDtypeStruct(ratio.shape, jnp.float32),
        in_specs=[SMEM, block(pad), block(planes), block(pad)],
        out_specs=block(planes),
        compiler_params=PARAMS,
        cost_estimate=pl.CostEstimate(
            flops=ratio.size * 2 * width * 6, bytes_accessed=12 * ratio.size, transcendentals=0
        ),
    )(kz, low, ratio, high)


def blur_back(low, u, high, ax, my, other):
    planes, rows, width = u.shape
    extra = [] if other is None else [other]
    return pl.pallas_call(
        back_kernel,
        out_shape=jax.ShapeDtypeStruct(u.shape, jnp.float32),
        in_specs=[VMEM] * (5 + len(extra)),
        out_specs=VMEM,
        scratch_shapes=[pltpu.VMEM((GROUP * (rows + 2 * low.shape[1]), width), jnp.float32)],
        compiler_params=PARAMS,
        cost_estimate=pl.CostEstimate(
            flops=u.size * 2 * width * 6, bytes_accessed=12 * u.size, transcendentals=0
        ),
    )(low, u, high, ax, my, *extra)


def banded(kern_row, outputs, inputs, shift):
    tap = jnp.arange(inputs)[None, :] - jnp.arange(outputs)[:, None] + shift
    taps = jnp.arange(kern_row.shape[0])
    return jnp.sum(jnp.where(tap[None] == taps[:, None, None], kern_row[:, None, None], 0.0), axis=0)


def x_matrix(kern_row, rows, pad):
    one = banded(kern_row, rows, rows + 2 * pad, 0)
    eye = jnp.eye(GROUP, dtype=jnp.float32)
    return (eye[:, None, :, None] * one[None, :, None, :]).reshape(
        GROUP * rows, GROUP * (rows + 2 * pad)
    )


def on_device(sections, count, views_data, start, psf_table, psf_index):
    slab = views_data[0]
    planes, width_x, width_y = start.shape
    pad = (psf_table.shape[2] - 1) // 2
    share = width_x // 4
    half = planes // 2
    view, gz = lax.axis_index("view"), lax.axis_index("gz")
    a, c, b = view // 2, view % 2, gz % 2

    def strip_of(a, b):
        return 2 * a + (a + b) % 2

    def move(value, target):
        pairs = []
        for v in range(sections):
            for g in range(count):
                to = target(v // 2, v % 2, g // 2, g % 2)
                if to is not None:
                    pairs.append((v * count + g, (2 * to[0] + to[1]) * count + 2 * to[2] + to[3]))
        return lax.ppermute(value, AXES, pairs)

    def along_z(step):
        def target(a, c, k, b):
            return (a, c, k + step, b) if 0 <= k + step < count // 2 else None

        return target

    def along_x(step):
        def target(a, c, k, b):
            strip = strip_of(a, b) + step
            if not 0 <= strip < 4:
                return None
            return (strip // 2, c, k, (strip % 2 + strip // 2) % 2)

        return target

    partners = (
        lambda a, c, k, b: (a, c, k, 1 - b),
        lambda a, c, k, b: (1 - a, c, k, b),
        lambda a, c, k, b: (1 - a, c, k, 1 - b),
    )
    core_swap = lambda a, c, k, b: (a, 1 - c, k, b)

    def rows_for(block, a, b):
        return lax.dynamic_slice_in_dim(block, strip_of(a, b) * share, share, 1)

    def in_order(first_is_mine, mine, theirs):
        return jnp.concatenate(
            [jnp.where(first_is_mine, mine, theirs), jnp.where(first_is_mine, theirs, mine)], axis=0
        )

    kern = jnp.sum(jnp.where(jnp.arange(psf_table.shape[0])[:, None, None] == psf_index[0], psf_table, 0.0), axis=0)
    kern = kern / jnp.sum(kern, axis=-1, keepdims=True)
    other = move(kern, partners[1])
    kerns = (jnp.where(a == 0, kern, other), jnp.where(a == 0, other, kern))
    setups = []
    for kern in kerns:
        flipped = kern[:, ::-1]
        mat_y = banded(kern[2], width_y, width_y, pad)
        setups.append((
            kern[0], x_matrix(kern[1], share, pad), mat_y.T, x_matrix(flipped[1], share, pad), mat_y
        ))

    theirs = rows_for(start, a, 1 - b)
    part = move(lax.dynamic_slice_in_dim(theirs, c * half, half, 0), partners[0])
    theirs = in_order(c == 0, part, move(part, core_swap))
    estimate = in_order(b == 0, rows_for(start, a, b), theirs)

    mine = rows_for(slab, a, b)
    from_y = move(rows_for(slab, a, 1 - b), partners[0])
    from_x = move(rows_for(slab, 1 - a, b), partners[1])
    from_xy = move(rows_for(slab, 1 - a, 1 - b), partners[2])
    data = tuple(
        in_order(b == 0, jnp.where(a == high, mine, from_x), jnp.where(a == high, from_y, from_xy))
        for high in range(2)
    )

    for step in range(ITERS):
        low = move(estimate[:, share - pad:], along_x(1))
        high = move(estimate[:, :pad], along_x(-1))
        wide = jnp.concatenate([low, estimate, high], axis=1)
        low = move(wide[2 * planes - pad:], along_z(1))
        high = move(wide[:pad], along_z(-1))
        wide = jnp.concatenate([low, wide, high], axis=0)
        smeared = []
        for which in range(2):
            kz, ax, my = setups[which][:3]
            ratio = blur_forward(kz, wide, data[which], ax, my)
            low = move(ratio[2 * planes - pad:], along_z(1))
            high = move(ratio[:pad], along_z(-1))
            smeared.append((low, ratio, high))
        edges = []
        for which in range(2):
            u = smear(setups[which][0], *smeared[which])
            low = move(u[:, share - pad:], along_x(1))
            high = move(u[:, :pad], along_x(-1))
            edges.append((low, u, high))
        product = None
        for which in range(2):
            ax, my = setups[which][3:]
            product = blur_back(*edges[which], ax, my, product)
        total = product * move(product, core_swap)
        estimate = estimate * jnp.sqrt(jnp.sqrt(total))

    def piece(b):
        return lax.dynamic_slice_in_dim(estimate, planes * b + half * c, half, 0)

    got = (
        piece(b),
        move(piece(1 - b), partners[0]),
        move(piece(b), partners[1]),
        move(piece(1 - b), partners[2]),
    )
    strips = []
    for strip in range(4):
        at_a = strip // 2
        at_b = (strip % 2 + at_a) % 2
        same_a, same_b = a == at_a, b == at_b
        strips.append(jnp.where(
            same_a, jnp.where(same_b, got[0], got[1]), jnp.where(same_b, got[2], got[3])
        ))
    whole = jnp.concatenate(strips, axis=1)
    return in_order(c == 0, whole, move(whole, core_swap))


def solution(mesh):
    return jax.shard_map(
        functools.partial(on_device, mesh.shape["view"], mesh.shape["gz"]),
        mesh=mesh,
        in_specs=(P("view", "gz", None, None), P("gz", None, None), P(), P("view")),
        out_specs=P("gz", None, None),
        check_vma=False,
    )
```

time: 626 us -> 278 us (0.44); the launches traced: 617 us -> 277 us
  waiting for transfers between devices: 348 us -> 99.8 us
  matrix products: 110 us -> 0 us
  Pallas kernels: 0 us -> 62.9 us
  blocking collectives: 39.4 us -> 0 us
  starting transfers between devices: 40 us -> 78.8 us
  other arithmetic: 45.4 us -> 16.7 us
  between operations: 14.7 us -> 1.51 us
    ppermute x8 -> x36, waiting for transfers between devices: 262 us -> 99.8 us  [move(): return lax.ppermute(value, AXES, pairs)]
    dot_general x8 -> x0, matrix products: 110 us -> none  [the longest x2 65.3 us: back_planes(): jnp.einsum('ij,ziy->zjy', mat_x, volume, precision=lax.Precision.HIGHEST)]
    pallas_call x0 -> x12, Pallas kernels: none -> 62.9 us  [the longest x4 31.4 us: blur_forward(): pl.pallas_call(forward_kernel, out_shape=jax.ShapeDtypeStruct(data.shape,...]
    ppermute x8 -> x36, starting transfers between devices: 26.5 us -> 78.8 us  [move(): return lax.ppermute(value, AXES, pairs)]
    all_gather x2 -> x0, waiting for transfers between devices: 49.4 us -> none  [on_device(): estimate = lax.all_gather(updated, 'view', axis=1, tiled=True)]
    all_to_all x1 -> x0, blocking collectives: 39.4 us -> none  [on_device(): lax.all_to_all(correction[None], 'view', split_axis=2, concat_axis=0, til...]
    div x2 -> x0, other arithmetic: 38.4 us -> none  [on_device(): ratio = slab / blurred]
    all_to_all x1 -> x0, waiting for transfers between devices: 36.9 us -> none  [on_device(): lax.all_to_all(correction[None], 'view', split_axis=2, concat_axis=0, til...]
  transfers between devices with their start and end apart: 11 -> 36, of which waited for: 9 -> 17; matrix products, arithmetic and copies ran while one was open for 0% -> 7% of each run, Pallas kernels for 0% -> 13%
where the time goes in v1:
time: 278 us; the launch traced here: 277 us
  waiting for transfers between devices  99.8 us (36%)
  starting transfers between devices  78.8 us (28%)
  Pallas kernels  62.9 us (23%)
  local copies, waits for them, and re-layouts  17.2 us (6%)
  other arithmetic  16.7 us (6%)
    ppermute x36, waiting for transfers between devices, move(): return lax.ppermute(value, AXES, pairs)  99.8 us
    ppermute x36, starting transfers between devices, move(): return lax.ppermute(value, AXES, pairs)  78.8 us
    pallas_call x4, Pallas kernels, blur_forward(): pl.pallas_call(forward_kernel, out_shape=jax.ShapeDtypeStruct(data.shape,...  31.4 us
    pallas_call x4, Pallas kernels, blur_back(): pl.pallas_call(back_kernel, out_shape=jax.ShapeDtypeStruct(u.shape, jnp.f...  20.8 us
    pallas_call x4, Pallas kernels, smear(): pl.pallas_call(smear_kernel, grid=(rows // 8,), out_shape=jax.ShapeDtypeS...  10.7 us
  transfers between devices with their start and end apart: 36, of which 17 were waited for; matrix products, arithmetic and copies ran while one was open for 7% of the time, Pallas kernels for 13%

profile of v1, /device:TPU:0, one launch (start us, length us, event | category | flops | bytes accessed | tf_op | source)
XLA Modules:
  0.0 276.9 jit_solution(1236903080191966282)
XLA Ops:
  1.6 3.0 %collective-permute-start.2 = (f32[3,17]{1,0:T(4,128)S(1)}, f32[3,17]{1,0:T(4,128)S(1)}, u32[]{:S(2)}, u32[]{:S(2)}) collective-permute-start(f32[3,17]{1,0:T(4,128)S(1)} %broadcast_divide_fusion), channel_id=1, source_target_pairs={{0,16},{1,17},{2,18},{3,19},{4,20},{5,21},{6,22},{7,23},{8,24},{9,... | collective-permute-start | bytes 620 | tf_op jit(solution)/shard_map/ppermute | solution.py:173
  5.7 1.6 collective-permute-start
  7.3 3.1 %dynamic-slice_bitcast_fusion.2 = (f32[16,32,384]{2,1,0:T(8,128)}, f32[16,32,384]{2,1,0:T(8,128)}, f32[16,32,384]{2,1,0:T(8,128)}) fusion(f32[1,16,128,384]{3,2,1,0:T(8,128)} %param.4, s32[]{:T(128)S(6)} %select_n.244, s32[]{:T(128)S(6)} %select_n.247, s32[]{:T(128)S(6)} %select_n.233), kind=kLoop, calls=%fused_computation.21 | loop fusion | bytes 4718604 | tf_op jit(solution)/shard_map/dynamic_slice | solution.py:198
  10.8 1.5 collective-permute-start.9
  12.3 1.5 collective-permute-start.8
  13.9 3.8 %collective-permute-done = f32[8,32,384]{2,1,0:T(8,128)S(1)} collective-permute-done((f32[8,32,384]{2,1,0:T(8,128)S(1)}, f32[8,32,384]{2,1,0:T(8,128)S(1)}, u32[]{:S(2)}, u32[]{:S(2)}) %collective-permute-start) | collective-permute-done | bytes 393248 | tf_op jit(solution)/shard_map/ppermute | solution.py:173
  19.5 1.3 dynamic-slice_select_fusion.1
  20.9 3.4 %collective-permute-start.3 = (f32[32,8,384]{2,1,0:T(8,128)S(1)}, f32[32,8,384]{2,1,0:T(8,128)S(1)}, u32[]{:S(2)}, u32[]{:S(2)}) collective-permute-start(f32[32,8,384]{2,1,0:T(8,128)S(1)} %get-tuple-element.52), channel_id=1, source_target_pairs={{0,1},{1,17},{2,3},{3,19},{4,5},{5,21},{6,7},{7,23},{8,9},{9,25},{... | collective-permute-start | bytes 1179656 | tf_op jit(solution)/shard_map/ppermute | solution.py:173
  24.3 1.3 collective-permute-start.4
  25.6 1.7 select_reduce_fusion
  27.3 30.1 %collective-permute-done.3 = f32[32,8,384]{2,1,0:T(8,128)S(1)} collective-permute-done((f32[32,8,384]{2,1,0:T(8,128)S(1)}, f32[32,8,384]{2,1,0:T(8,128)S(1)}, u32[]{:S(2)}, u32[]{:S(2)}) %collective-permute-start.3) | collective-permute-done | bytes 393248 | tf_op jit(solution)/shard_map/ppermute | solution.py:173
  59.7 4.3 %collective-permute-start.5 = (f32[8,48,384]{2,1,0:T(8,128)}, f32[8,48,384]{2,1,0:T(8,128)}, u32[]{:S(2)}, u32[]{:S(2)}) collective-permute-start(f32[8,48,384]{2,1,0:T(8,128)} %get-tuple-element.26), channel_id=1, source_target_pairs={{0,2},{1,3},{2,4},{3,5},{4,6},{5,7},{8,10},{9,11},{10,12},{11,13},... | collective-permute-start | bytes 1769480 | tf_op jit(solution)/shard_map/ppermute | solution.py:173
  64.0 1.3 collective-permute-start.6
  68.6 2.0 broadcast_select_fusion.5
  70.9 4.0 %collective-permute-done.5 = f32[8,48,384]{2,1,0:T(8,128)} collective-permute-done((f32[8,48,384]{2,1,0:T(8,128)}, f32[8,48,384]{2,1,0:T(8,128)}, u32[]{:S(2)}, u32[]{:S(2)}) %collective-permute-start.5) | collective-permute-done | bytes 589856 | tf_op jit(solution)/shard_map/ppermute | solution.py:173
  74.9 4.9 %collective-permute-done.6 = f32[8,48,384]{2,1,0:T(8,128)} collective-permute-done((f32[8,48,384]{2,1,0:T(8,128)}, f32[8,48,384]{2,1,0:T(8,128)}, u32[]{:S(2)}, u32[]{:S(2)}) %collective-permute-start.6) | collective-permute-done | bytes 589856 | tf_op jit(solution)/shard_map/ppermute | solution.py:173
  79.8 1.5 pad_maximum_fusion.e_ref
  81.4 7.8 %shard_map.48.r_ref = f32[32,32,384]{2,1,0:T(8,128)S(1)} custom-call(f32[17]{0:T(128)S(1)} %get-tuple-element.62.kz_ref, f32[48,48,384]{2,1,0:T(8,128)S(1)} %pad_maximum_fusion.e_ref, f32[32,32,384]{2,1,0:T(8,128)S(1)} %get-tuple-element.75.d_ref, f32[128,192]{1,0:T(8,128)S(1)} %copy-done.8, f32[384,384]{1,0:T(8,128)S(1)} %bitcast.37), custom_call_target="tpu_custom_call" | custom-call | flops 3623878656 | bytes 6291456 | tf_op jit(solution)/shard_map/pallas_call | solution.py:94
  89.3 1.3 collective-permute-start.15
  90.6 4.6 %collective-permute-start.14 = (f32[8,32,384]{2,1,0:T(8,128)S(1)}, f32[8,32,384]{2,1,0:T(8,128)S(1)}, u32[]{:S(2)}, u32[]{:S(2)}) collective-permute-start(f32[8,32,384]{2,1,0:T(8,128)S(1)} %get-tuple-element.47), channel_id=1, source_target_pairs={{0,2},{1,3},{2,4},{3,5},{4,6},{5,7},{8,10},{9,11},{10,12},{11,13},... | collective-permute-start | bytes 1179656 | tf_op jit(solution)/shard_map/ppermute | solution.py:173
  95.2 7.8 %shard_map.46.r_ref = f32[32,32,384]{2,1,0:T(8,128)S(1)} custom-call(f32[17]{0:T(128)S(1)} %get-tuple-element.70.kz_ref, f32[48,48,384]{2,1,0:T(8,128)S(1)} %pad_maximum_fusion.e_ref, f32[32,32,384]{2,1,0:T(8,128)S(1)} %get-tuple-element.74.d_ref, f32[128,192]{1,0:T(8,128)S(1)} %mul.129.ax_ref, f32[384,384]{1,0:T(8,128)S(1)} %bitcast.35), custom_call_target="tpu_custom_call" | custom-call | flops 3623878656 | bytes 6291456 | tf_op jit(solution)/shard_map/pallas_call | solution.py:94
  103.1 1.3 collective-permute-start.11
  104.4 4.6 %collective-permute-start.10 = (f32[8,32,384]{2,1,0:T(8,128)S(1)}, f32[8,32,384]{2,1,0:T(8,128)S(1)}, u32[]{:S(2)}, u32[]{:S(2)}) collective-permute-start(f32[8,32,384]{2,1,0:T(8,128)S(1)} %get-tuple-element.51), channel_id=1, source_target_pairs={{0,2},{1,3},{2,4},{3,5},{4,6},{5,7},{8,10},{9,11},{10,12},{11,13},... | collective-permute-start | bytes 1179656 | tf_op jit(solution)/shard_map/ppermute | solution.py:173
  109.0 2.7 shard_map.49.u_ref
  113.8 1.3 collective-permute-start.17
  115.1 5.3 %collective-permute-start.16 = (f32[32,8,384]{2,1,0:T(8,128)}, f32[32,8,384]{2,1,0:T(8,128)}, u32[]{:S(2)}, u32[]{:S(2)}) collective-permute-start(f32[32,8,384]{2,1,0:T(8,128)} %get-tuple-element.45), channel_id=1, source_target_pairs={{0,1},{1,17},{2,3},{3,19},{4,5},{5,21},{6,7},{7,23},{8,9},{9,25},{... | collective-permute-start | bytes 1179656 | tf_op jit(solution)/shard_map/ppermute | solution.py:173
  120.4 2.7 shard_map.47.u_ref
  125.2 1.3 collective-permute-start.13
  126.5 5.3 %collective-permute-start.12 = (f32[32,8,384]{2,1,0:T(8,128)}, f32[32,8,384]{2,1,0:T(8,128)}, u32[]{:S(2)}, u32[]{:S(2)}) collective-permute-start(f32[32,8,384]{2,1,0:T(8,128)} %get-tuple-element.49), channel_id=1, source_target_pairs={{0,1},{1,17},{2,3},{3,19},{4,5},{5,21},{6,7},{7,23},{8,9},{9,25},{... | collective-permute-start | bytes 1179656 | tf_op jit(solution)/shard_map/ppermute | solution.py:173
  131.8 1.8 mul.138.ax_ref
  133.5 1.8 mul.132.ax_ref
  135.3 1.4 copy-done.5
  137.6 5.8 %shard_map.50.rest_0_ = f32[32,32,384]{2,1,0:T(8,128)S(1)} custom-call(f32[32,8,384]{2,1,0:T(8,128)} %collective-permute-done.16.low_ref, f32[32,32,384]{2,1,0:T(8,128)S(1)} %copy-done.5, f32[32,8,384]{2,1,0:T(8,128)} %collective-permute-done.17.high_ref, f32[128,192]{1,0:T(8,128)S(1)} %copy-done.11, f32[384,384]{1,0:T(8,128)S(1)} %get-tuple-element.5.my_ref), custom_call_target="tpu_custom_call" | custom-call | flops 1811939328 | bytes 4718592 | tf_op jit(solution)/shard_map/pallas_call | solution.py:127
  143.5 5.8 %shard_map.51 = f32[32,32,384]{2,1,0:T(8,128)S(1)} custom-call(f32[32,8,384]{2,1,0:T(8,128)} %collective-permute-done.12.low_ref, f32[32,32,384]{2,1,0:T(8,128)S(1)} %copy-done.7, f32[32,8,384]{2,1,0:T(8,128)} %collective-permute-done.13.high_ref, f32[128,192]{1,0:T(8,128)S(1)} %copy-done.10, f32[384,384]{1,0:T(8,128)S(1)} %get-tuple-element.6.my_ref, ...), custom_call_target="tpu_custom_call" | custom-call | flops 1811939328 | bytes 4718592 | tf_op jit(solution)/shard_map/pallas_call | solution.py:127
  149.4 3.4 %collective-permute-done.18 = f32[32,32,384]{2,1,0:T(8,128)S(1)} collective-permute-done((f32[32,32,384]{2,1,0:T(8,128)S(1)}, f32[32,32,384]{2,1,0:T(8,128)S(1)}, u32[]{:S(2)}, u32[]{:S(2)}) %collective-permute-start.18) | collective-permute-done | bytes 1572896 | tf_op jit(solution)/shard_map/ppermute | solution.py:173
  153.7 2.3 collective-permute-start.19
  156.0 1.3 collective-permute-start.20
  157.3 7.3 %collective-permute-done.19 = f32[32,8,384]{2,1,0:T(8,128)S(1)} collective-permute-done((f32[32,8,384]{2,1,0:T(8,128)S(1)}, f32[32,8,384]{2,1,0:T(8,128)S(1)}, u32[]{:S(2)}, u32[]{:S(2)}) %collective-permute-start.19) | collective-permute-done | bytes 393248 | tf_op jit(solution)/shard_map/ppermute | solution.py:173
  164.6 4.3 %collective-permute-done.20 = f32[32,8,384]{2,1,0:T(8,128)S(1)} collective-permute-done((f32[32,8,384]{2,1,0:T(8,128)S(1)}, f32[32,8,384]{2,1,0:T(8,128)S(1)}, u32[]{:S(2)}, u32[]{:S(2)}) %collective-permute-start.20) | collective-permute-done | bytes 393248 | tf_op jit(solution)/shard_map/ppermute | solution.py:173
  169.0 2.7 collective-permute-start.21
  171.7 1.4 collective-permute-start.22
  173.2 10.4 %collective-permute-done.21 = f32[8,48,384]{2,1,0:T(8,128)S(1)} collective-permute-done((f32[8,48,384]{2,1,0:T(8,128)S(1)}, f32[8,48,384]{2,1,0:T(8,128)S(1)}, u32[]{:S(2)}, u32[]{:S(2)}) %collective-permute-start.21) | collective-permute-done | bytes 589856 | tf_op jit(solution)/shard_map/ppermute | solution.py:173
  183.5 4.3 %collective-permute-done.22 = f32[8,48,384]{2,1,0:T(8,128)S(1)} collective-permute-done((f32[8,48,384]{2,1,0:T(8,128)S(1)}, f32[8,48,384]{2,1,0:T(8,128)S(1)}, u32[]{:S(2)}, u32[]{:S(2)}) %collective-permute-start.22) | collective-permute-done | bytes 589856 | tf_op jit(solution)/shard_map/ppermute | solution.py:173
  188.1 7.8 %shard_map.54.r_ref = f32[32,32,384]{2,1,0:T(8,128)S(1)} custom-call(f32[17]{0:T(128)S(1)} %get-tuple-element.62.kz_ref, f32[48,48,384]{2,1,0:T(8,128)S(1)} %pad_maximum_fusion.1.e_ref, f32[32,32,384]{2,1,0:T(8,128)S(1)} %copy-done.1, f32[128,192]{1,0:T(8,128)S(1)} %copy-done.9, f32[384,384]{1,0:T(8,128)S(1)} %bitcast.38), custom_call_target="tpu_custom_call" | custom-call | flops 3623878656 | bytes 6291456 | tf_op jit(solution)/shard_map/pallas_call | solution.py:94
  196.1 1.3 collective-permute-start.28
  197.4 4.6 %collective-permute-start.27 = (f32[8,32,384]{2,1,0:T(8,128)S(1)}, f32[8,32,384]{2,1,0:T(8,128)S(1)}, u32[]{:S(2)}, u32[]{:S(2)}) collective-permute-start(f32[8,32,384]{2,1,0:T(8,128)S(1)} %get-tuple-element.37), channel_id=1, source_target_pairs={{0,2},{1,3},{2,4},{3,5},{4,6},{5,7},{8,10},{9,11},{10,12},{11,13},... | collective-permute-start | bytes 1179656 | tf_op jit(solution)/shard_map/ppermute | solution.py:173
  201.9 7.8 %shard_map.52.r_ref = f32[32,32,384]{2,1,0:T(8,128)S(1)} custom-call(f32[17]{0:T(128)S(1)} %get-tuple-element.70.kz_ref, f32[48,48,384]{2,1,0:T(8,128)S(1)} %pad_maximum_fusion.1.e_ref, f32[32,32,384]{2,1,0:T(8,128)S(1)} %get-tuple-element.74.d_ref, f32[128,192]{1,0:T(8,128)S(1)} %mul.129.ax_ref, f32[384,384]{1,0:T(8,128)S(1)} %bitcast.36), custom_call_target="tpu_custom_call" | custom-call | flops 3623878656 | bytes 6291456 | tf_op jit(solution)/shard_map/pallas_call | solution.py:94
  209.8 1.3 collective-permute-start.24
  211.1 4.6 %collective-permute-start.23 = (f32[8,32,384]{2,1,0:T(8,128)S(1)}, f32[8,32,384]{2,1,0:T(8,128)S(1)}, u32[]{:S(2)}, u32[]{:S(2)}) collective-permute-start(f32[8,32,384]{2,1,0:T(8,128)S(1)} %get-tuple-element.41), channel_id=1, source_target_pairs={{0,2},{1,3},{2,4},{3,5},{4,6},{5,7},{8,10},{9,11},{10,12},{11,13},... | collective-permute-start | bytes 1179656 | tf_op jit(solution)/shard_map/ppermute | solution.py:173
  215.7 2.7 shard_map.55.u_ref
  218.5 1.3 collective-permute-start.30
  219.8 4.6 %collective-permute-start.29 = (f32[32,8,384]{2,1,0:T(8,128)S(1)}, f32[32,8,384]{2,1,0:T(8,128)S(1)}, u32[]{:S(2)}, u32[]{:S(2)}) collective-permute-start(f32[32,8,384]{2,1,0:T(8,128)S(1)} %get-tuple-element.35), channel_id=1, source_target_pairs={{0,1},{1,17},{2,3},{3,19},{4,5},{5,21},{6,7},{7,23},{8,9},{9,25},{... | collective-permute-start | bytes 1179656 | tf_op jit(solution)/shard_map/ppermute | solution.py:173
  224.4 2.7 shard_map.53.u_ref
  227.2 1.3 collective-permute-start.26
  228.5 4.6 %collective-permute-start.25 = (f32[32,8,384]{2,1,0:T(8,128)S(1)}, f32[32,8,384]{2,1,0:T(8,128)S(1)}, u32[]{:S(2)}, u32[]{:S(2)}) collective-permute-start(f32[32,8,384]{2,1,0:T(8,128)S(1)} %get-tuple-element.39), channel_id=1, source_target_pairs={{0,1},{1,17},{2,3},{3,19},{4,5},{5,21},{6,7},{7,23},{8,9},{9,25},{... | collective-permute-start | bytes 1179656 | tf_op jit(solution)/shard_map/ppermute | solution.py:173
  233.1 4.6 %shard_map.56.rest_0_ = f32[32,32,384]{2,1,0:T(8,128)S(1)} custom-call(f32[32,8,384]{2,1,0:T(8,128)S(1)} %collective-permute-done.29.low_ref, f32[32,32,384]{2,1,0:T(8,128)S(1)} %shard_map.55.u_ref, f32[32,8,384]{2,1,0:T(8,128)S(1)} %collective-permute-done.30.high_ref, f32[128,192]{1,0:T(8,128)S(1)} %copy-done.12, f32[384,384]{1,0:T(8,128)S(1)} %get-tuple-element.5.my_ref), custom_call_target="tpu_custom_call" | custom-call | flops 1811939328 | bytes 4718592 | tf_op jit(solution)/shard_map/pallas_call | solution.py:127
  238.3 4.6 %shard_map.57 = f32[32,32,384]{2,1,0:T(8,128)S(1)} custom-call(f32[32,8,384]{2,1,0:T(8,128)S(1)} %collective-permute-done.25.low_ref, f32[32,32,384]{2,1,0:T(8,128)S(1)} %shard_map.53.u_ref, f32[32,8,384]{2,1,0:T(8,128)S(1)} %collective-permute-done.26.high_ref, f32[128,192]{1,0:T(8,128)S(1)} %copy-done.10, f32[384,384]{1,0:T(8,128)S(1)} %get-tuple-element.6.my_ref, ...), custom_call_target="tpu_custom_call" | custom-call | flops 1811939328 | bytes 4718592 | tf_op jit(solution)/shard_map/pallas_call | solution.py:127
  243.0 3.5 %collective-permute-done.31 = f32[32,32,384]{2,1,0:T(8,128)} collective-permute-done((f32[32,32,384]{2,1,0:T(8,128)S(1)}, f32[32,32,384]{2,1,0:T(8,128)}, u32[]{:S(2)}, u32[]{:S(2)}) %collective-permute-start.31) | collective-permute-done | bytes 1572896 | tf_op jit(solution)/shard_map/ppermute | solution.py:173
  246.5 2.7 sqrt_multiply_fusion
  249.3 3.5 %collective-permute-start.34 = (f32[8,32,384]{2,1,0:T(8,128)S(1)}, f32[8,32,384]{2,1,0:T(8,128)S(1)}, u32[]{:S(2)}, u32[]{:S(2)}) collective-permute-start(f32[8,32,384]{2,1,0:T(8,128)S(1)} %get-tuple-element.32), channel_id=1, source_target_pairs={{0,17},{1,16},{2,19},{3,18},{4,21},{5,20},{6,23},{7,22},{8,25},{9,... | collective-permute-start | bytes 1179656 | tf_op jit(solution)/shard_map/ppermute | solution.py:173
  253.5 9.4 %collective-permute-done.34 = f32[8,32,384]{2,1,0:T(8,128)S(1)} collective-permute-done((f32[8,32,384]{2,1,0:T(8,128)S(1)}, f32[8,32,384]{2,1,0:T(8,128)S(1)}, u32[]{:S(2)}, u32[]{:S(2)}) %collective-permute-start.34) | collective-permute-done | bytes 393248 | tf_op jit(solution)/shard_map/ppermute | solution.py:173
  262.8 7.8 %collective-permute-done.32 = f32[8,32,384]{2,1,0:T(8,128)S(1)} collective-permute-done((f32[8,32,384]{2,1,0:T(8,128)S(1)}, f32[8,32,384]{2,1,0:T(8,128)S(1)}, u32[]{:S(2)}, u32[]{:S(2)}) %collective-permute-start.32) | collective-permute-done | bytes 393248 | tf_op jit(solution)/shard_map/ppermute | solution.py:173
  271.3 3.4 %collective-permute-done.35 = f32[8,128,384]{2,1,0:T(8,128)S(1)} collective-permute-done((f32[8,128,384]{2,1,0:T(8,128)S(1)}, f32[8,128,384]{2,1,0:T(8,128)S(1)}, u32[]{:S(2)}, u32[]{:S(2)}) %collective-permute-start.35) | collective-permute-done | bytes 1572896 | tf_op jit(solution)/shard_map/ppermute | solution.py:173
  275.0 1.9 pad_maximum_fusion.2
  (114 shorter events, 19.2 us)
Async XLA Ops:
  1.6 16.1 %collective-permute-start.2 = (f32[3,17]{1,0:T(4,128)S(1)}, f32[3,17]{1,0:T(4,128)S(1)}, u32[]{:S(2)}, u32[]{:S(2)}) collective-permute-start(f32[3,17]{1,0:T(4,128)S(1)} %broadcast_divide_fusion), channel_id=1, source_target_pairs={{0,16},{1,17},{2,18},{3,19},{4,20},{5,21},{6,22},{7,23},{8,24},{9,... | collective-permute-start | bytes 620 | tf_op jit(solution)/shard_map/ppermute | solution.py:173
  5.7 12.1 %collective-permute-start = (f32[8,32,384]{2,1,0:T(8,128)S(1)}, f32[8,32,384]{2,1,0:T(8,128)S(1)}, u32[]{:S(2)}, u32[]{:S(2)}) collective-permute-start(f32[8,32,384]{2,1,0:T(8,128)S(1)} %constant_dynamic-slice_fusion.2), channel_id=1, source_target_pairs={{0,1},{1,0},{2,3},{3,2},{4,5},{5,4},{6,7},{7,6},{8,9},{9,8},{10,11... | collective-permute-start | bytes 1179656 | tf_op jit(solution)/shard_map/ppermute | solution.py:173
  10.3 58.2 %collective-permute-start.7 = (f32[16,32,384]{2,1,0:T(8,128)}, f32[16,32,384]{2,1,0:T(8,128)S(1)}, u32[]{:S(2)}, u32[]{:S(2)}) collective-permute-start(f32[16,32,384]{2,1,0:T(8,128)} %get-tuple-element.21), channel_id=1, source_target_pairs={{0,16},{1,17},{2,18},{3,19},{4,20},{5,21},{6,22},{7,23},{8,24},{9,... | collective-permute-start | bytes 2359304 | tf_op jit(solution)/shard_map/ppermute | solution.py:173
  10.8 57.7 %collective-permute-start.9 = (f32[16,32,384]{2,1,0:T(8,128)}, f32[16,32,384]{2,1,0:T(8,128)}, u32[]{:S(2)}, u32[]{:S(2)}) collective-permute-start(f32[16,32,384]{2,1,0:T(8,128)} %get-tuple-element.22), channel_id=1, source_target_pairs={{0,17},{1,16},{2,19},{3,18},{4,21},{5,20},{6,23},{7,22},{8,25},{9,... | collective-permute-start | bytes 2359304 | tf_op jit(solution)/shard_map/ppermute | solution.py:173
  12.3 56.3 %collective-permute-start.8 = (f32[16,32,384]{2,1,0:T(8,128)}, f32[16,32,384]{2,1,0:T(8,128)}, u32[]{:S(2)}, u32[]{:S(2)}) collective-permute-start(f32[16,32,384]{2,1,0:T(8,128)} %get-tuple-element.23), channel_id=1, source_target_pairs={{0,1},{1,0},{2,3},{3,2},{4,5},{5,4},{6,7},{7,6},{8,9},{9,8},{10,11... | collective-permute-start | bytes 2359304 | tf_op jit(solution)/shard_map/ppermute | solution.py:173
  17.7 1.7 collective-permute-start.1
  20.8 37.7 %copy-start.14 = (f32[16,32,384]{2,1,0:T(8,128)}, f32[16,32,384]{2,1,0:T(8,128)S(1)}, u32[]{:S(2)}) copy-start(f32[16,32,384]{2,1,0:T(8,128)S(1)} %get-tuple-element.17) | copy-start | bytes 2359300
  20.8 37.6 %copy-start.17 = (f32[16,32,384]{2,1,0:T(8,128)}, f32[16,32,384]{2,1,0:T(8,128)S(1)}, u32[]{:S(2)}) copy-start(f32[16,32,384]{2,1,0:T(8,128)S(1)} %get-tuple-element.18) | copy-start | bytes 2359300
  20.9 36.6 %collective-permute-start.3 = (f32[32,8,384]{2,1,0:T(8,128)S(1)}, f32[32,8,384]{2,1,0:T(8,128)S(1)}, u32[]{:S(2)}, u32[]{:S(2)}) collective-permute-start(f32[32,8,384]{2,1,0:T(8,128)S(1)} %get-tuple-element.52), channel_id=1, source_target_pairs={{0,1},{1,17},{2,3},{3,19},{4,5},{5,21},{6,7},{7,23},{8,9},{9,25},{... | collective-permute-start | bytes 1179656 | tf_op jit(solution)/shard_map/ppermute | solution.py:173
  24.3 34.1 %collective-permute-start.4 = (f32[32,8,384]{2,1,0:T(8,128)S(1)}, f32[32,8,384]{2,1,0:T(8,128)S(1)}, u32[]{:S(2)}, u32[]{:S(2)}) collective-permute-start(f32[32,8,384]{2,1,0:T(8,128)S(1)} %get-tuple-element.53), channel_id=1, source_target_pairs={{1,0},{3,2},{5,4},{7,6},{9,8},{11,10},{13,12},{15,14},{16,17},{17,... | collective-permute-start | bytes 1179656 | tf_op jit(solution)/shard_map/ppermute | solution.py:173
  57.5 2.2 copy-start.20
  58.4 1.2 copy-start.22
  59.7 15.2 %collective-permute-start.5 = (f32[8,48,384]{2,1,0:T(8,128)}, f32[8,48,384]{2,1,0:T(8,128)}, u32[]{:S(2)}, u32[]{:S(2)}) collective-permute-start(f32[8,48,384]{2,1,0:T(8,128)} %get-tuple-element.26), channel_id=1, source_target_pairs={{0,2},{1,3},{2,4},{3,5},{4,6},{5,7},{8,10},{9,11},{10,12},{11,13},... | collective-permute-start | bytes 1769480 | tf_op jit(solution)/shard_map/ppermute | solution.py:173
  64.0 15.9 %collective-permute-start.6 = (f32[8,48,384]{2,1,0:T(8,128)}, f32[8,48,384]{2,1,0:T(8,128)}, u32[]{:S(2)}, u32[]{:S(2)}) collective-permute-start(f32[8,48,384]{2,1,0:T(8,128)} %get-tuple-element.27), channel_id=1, source_target_pairs={{2,0},{3,1},{4,2},{5,3},{6,4},{7,5},{10,8},{11,9},{12,10},{13,11},... | collective-permute-start | bytes 1769480 | tf_op jit(solution)/shard_map/ppermute | solution.py:173
  70.6 9.2 %copy-start.15 = (f32[16,32,384]{2,1,0:T(8,128)S(1)}, f32[16,32,384]{2,1,0:T(8,128)}, u32[]{:S(2)}) copy-start(f32[16,32,384]{2,1,0:T(8,128)} %copy-done.14) | copy-start | bytes 2359300
  70.6 9.2 %copy-start.18 = (f32[16,32,384]{2,1,0:T(8,128)S(1)}, f32[16,32,384]{2,1,0:T(8,128)}, u32[]{:S(2)}) copy-start(f32[16,32,384]{2,1,0:T(8,128)} %copy-done.17) | copy-start | bytes 2359300
  70.6 9.2 %copy-start.21 = (f32[32,8,384]{2,1,0:T(8,128)S(1)}, f32[32,8,384]{2,1,0:T(8,128)}, u32[]{:S(2)}) copy-start(f32[32,8,384]{2,1,0:T(8,128)} %copy-done.20) | copy-start | bytes 1179652
  70.6 9.2 %copy-start.23 = (f32[32,8,384]{2,1,0:T(8,128)S(1)}, f32[32,8,384]{2,1,0:T(8,128)}, u32[]{:S(2)}) copy-start(f32[32,8,384]{2,1,0:T(8,128)} %copy-done.22) | copy-start | bytes 1179652
  70.9 10.5 %copy-start = (f32[32,32,384]{2,1,0:T(8,128)}, f32[32,32,384]{2,1,0:T(8,128)S(1)}, u32[]{:S(2)}) copy-start(f32[32,32,384]{2,1,0:T(8,128)S(1)} %get-tuple-element.75.d_ref) | copy-start | bytes 4718596
  70.9 10.5 %copy-start.2 = (f32[384,384]{0,1:T(8,128)S(1)}, f32[384,384]{0,1:T(8,128)}, u32[]{:S(2)}) copy-start(f32[384,384]{0,1:T(8,128)} %copy.14) | copy-start | bytes 1769476
  70.9 10.5 %copy-start.8 = (f32[128,192]{1,0:T(8,128)S(1)}, f32[128,192]{1,0:T(8,128)}, u32[]{:S(2)}) copy-start(f32[128,192]{1,0:T(8,128)} %mul.135.ax_ref) | copy-start | bytes 294916
  89.3 19.7 %collective-permute-start.15 = (f32[8,32,384]{2,1,0:T(8,128)S(1)}, f32[8,32,384]{2,1,0:T(8,128)S(1)}, u32[]{:S(2)}, u32[]{:S(2)}) collective-permute-start(f32[8,32,384]{2,1,0:T(8,128)S(1)} %get-tuple-element.46), channel_id=1, source_target_pairs={{2,0},{3,1},{4,2},{5,3},{6,4},{7,5},{10,8},{11,9},{12,10},{13,11},... | collective-permute-start | bytes 1179656 | tf_op jit(solution)/shard_map/ppermute | solution.py:173
  90.6 18.4 %collective-permute-start.14 = (f32[8,32,384]{2,1,0:T(8,128)S(1)}, f32[8,32,384]{2,1,0:T(8,128)S(1)}, u32[]{:S(2)}, u32[]{:S(2)}) collective-permute-start(f32[8,32,384]{2,1,0:T(8,128)S(1)} %get-tuple-element.47), channel_id=1, source_target_pairs={{0,2},{1,3},{2,4},{3,5},{4,6},{5,7},{8,10},{9,11},{10,12},{11,13},... | collective-permute-start | bytes 1179656 | tf_op jit(solution)/shard_map/ppermute | solution.py:173
  103.1 17.3 %collective-permute-start.11 = (f32[8,32,384]{2,1,0:T(8,128)S(1)}, f32[8,32,384]{2,1,0:T(8,128)S(1)}, u32[]{:S(2)}, u32[]{:S(2)}) collective-permute-start(f32[8,32,384]{2,1,0:T(8,128)S(1)} %get-tuple-element.50), channel_id=1, source_target_pairs={{2,0},{3,1},{4,2},{5,3},{6,4},{7,5},{10,8},{11,9},{12,10},{13,11},... | collective-permute-start | bytes 1179656 | tf_op jit(solution)/shard_map/ppermute | solution.py:173
  104.4 16.0 %collective-permute-start.10 = (f32[8,32,384]{2,1,0:T(8,128)S(1)}, f32[8,32,384]{2,1,0:T(8,128)S(1)}, u32[]{:S(2)}, u32[]{:S(2)}) collective-permute-start(f32[8,32,384]{2,1,0:T(8,128)S(1)} %get-tuple-element.51), channel_id=1, source_target_pairs={{0,2},{1,3},{2,4},{3,5},{4,6},{5,7},{8,10},{9,11},{10,12},{11,13},... | collective-permute-start | bytes 1179656 | tf_op jit(solution)/shard_map/ppermute | solution.py:173
  112.7 1.1 copy-start.4
  113.8 21.5 %collective-permute-start.17 = (f32[32,8,384]{2,1,0:T(8,128)}, f32[32,8,384]{2,1,0:T(8,128)}, u32[]{:S(2)}, u32[]{:S(2)}) collective-permute-start(f32[32,8,384]{2,1,0:T(8,128)} %get-tuple-element.44), channel_id=1, source_target_pairs={{1,0},{3,2},{5,4},{7,6},{9,8},{11,10},{13,12},{15,14},{16,17},{17,... | collective-permute-start | bytes 1179656 | tf_op jit(solution)/shard_map/ppermute | solution.py:173
  115.1 20.2 %collective-permute-start.16 = (f32[32,8,384]{2,1,0:T(8,128)}, f32[32,8,384]{2,1,0:T(8,128)}, u32[]{:S(2)}, u32[]{:S(2)}) collective-permute-start(f32[32,8,384]{2,1,0:T(8,128)} %get-tuple-element.45), channel_id=1, source_target_pairs={{0,1},{1,17},{2,3},{3,19},{4,5},{5,21},{6,7},{7,23},{8,9},{9,25},{... | collective-permute-start | bytes 1179656 | tf_op jit(solution)/shard_map/ppermute | solution.py:173
  124.0 1.1 copy-start.6
  125.2 18.3 %collective-permute-start.13 = (f32[32,8,384]{2,1,0:T(8,128)}, f32[32,8,384]{2,1,0:T(8,128)}, u32[]{:S(2)}, u32[]{:S(2)}) collective-permute-start(f32[32,8,384]{2,1,0:T(8,128)} %get-tuple-element.48), channel_id=1, source_target_pairs={{1,0},{3,2},{5,4},{7,6},{9,8},{11,10},{13,12},{15,14},{16,17},{17,... | collective-permute-start | bytes 1179656 | tf_op jit(solution)/shard_map/ppermute | solution.py:173
  126.5 17.0 %collective-permute-start.12 = (f32[32,8,384]{2,1,0:T(8,128)}, f32[32,8,384]{2,1,0:T(8,128)}, u32[]{:S(2)}, u32[]{:S(2)}) collective-permute-start(f32[32,8,384]{2,1,0:T(8,128)} %get-tuple-element.49), channel_id=1, source_target_pairs={{0,1},{1,17},{2,3},{3,19},{4,5},{5,21},{6,7},{7,23},{8,9},{9,25},{... | collective-permute-start | bytes 1179656 | tf_op jit(solution)/shard_map/ppermute | solution.py:173
  135.3 1.4 copy-start.5
  136.7 0.9 copy-start.11
  137.6 5.9 %copy-start.7 = (f32[32,32,384]{2,1,0:T(8,128)S(1)}, f32[32,32,384]{2,1,0:T(8,128)}, u32[]{:S(2)}) copy-start(f32[32,32,384]{2,1,0:T(8,128)} %copy-done.6) | copy-start | bytes 4718596
  137.6 5.9 %copy-start.10 = (f32[128,192]{1,0:T(8,128)S(1)}, f32[128,192]{1,0:T(8,128)}, u32[]{:S(2)}) copy-start(f32[128,192]{1,0:T(8,128)} %mul.132.ax_ref) | copy-start | bytes 294916
  143.5 9.4 %copy-start.16 = (f32[16,32,384]{2,1,0:T(8,128)S(1)}, f32[16,32,384]{2,1,0:T(8,128)}, u32[]{:S(2)}) copy-start(f32[16,32,384]{2,1,0:T(8,128)} %copy-done.14) | copy-start | bytes 2359300
  143.5 9.4 %copy-start.19 = (f32[16,32,384]{2,1,0:T(8,128)S(1)}, f32[16,32,384]{2,1,0:T(8,128)}, u32[]{:S(2)}) copy-start(f32[16,32,384]{2,1,0:T(8,128)} %copy-done.17) | copy-start | bytes 2359300
  149.4 3.5 %collective-permute-start.18 = (f32[32,32,384]{2,1,0:T(8,128)S(1)}, f32[32,32,384]{2,1,0:T(8,128)S(1)}, u32[]{:S(2)}, u32[]{:S(2)}) collective-permute-start(f32[32,32,384]{2,1,0:T(8,128)S(1)} %shard_map.51), channel_id=1, source_target_pairs={{0,8},{1,9},{2,10},{3,11},{4,12},{5,13},{6,14},{7,15},{8,0},{9,1},... | collective-permute-start | bytes 4718600 | tf_op jit(solution)/shard_map/ppermute | solution.py:173
  153.7 34.2 %copy-start.13 = (f32[32,32,384]{2,1,0:T(8,128)}, f32[32,32,384]{2,1,0:T(8,128)S(1)}, u32[]{:S(2)}) copy-start(f32[32,32,384]{2,1,0:T(8,128)S(1)} %fusion) | copy-start | bytes 4718596
  153.7 10.9 %collective-permute-start.19 = (f32[32,8,384]{2,1,0:T(8,128)S(1)}, f32[32,8,384]{2,1,0:T(8,128)S(1)}, u32[]{:S(2)}, u32[]{:S(2)}) collective-permute-start(f32[32,8,384]{2,1,0:T(8,128)S(1)} %get-tuple-element.42), channel_id=1, source_target_pairs={{0,1},{1,17},{2,3},{3,19},{4,5},{5,21},{6,7},{7,23},{8,9},{9,25},{... | collective-permute-start | bytes 1179656 | tf_op jit(solution)/shard_map/ppermute | solution.py:173
  156.0 12.9 %collective-permute-start.20 = (f32[32,8,384]{2,1,0:T(8,128)S(1)}, f32[32,8,384]{2,1,0:T(8,128)S(1)}, u32[]{:S(2)}, u32[]{:S(2)}) collective-permute-start(f32[32,8,384]{2,1,0:T(8,128)S(1)} %get-tuple-element.43), channel_id=1, source_target_pairs={{1,0},{3,2},{5,4},{7,6},{9,8},{11,10},{13,12},{15,14},{16,17},{17,... | collective-permute-start | bytes 1179656 | tf_op jit(solution)/shard_map/ppermute | solution.py:173
  169.0 14.5 %collective-permute-start.21 = (f32[8,48,384]{2,1,0:T(8,128)S(1)}, f32[8,48,384]{2,1,0:T(8,128)S(1)}, u32[]{:S(2)}, u32[]{:S(2)}) collective-permute-start(f32[8,48,384]{2,1,0:T(8,128)S(1)} %get-tuple-element.24), channel_id=1, source_target_pairs={{0,2},{1,3},{2,4},{3,5},{4,6},{5,7},{8,10},{9,11},{10,12},{11,13},... | collective-permute-start | bytes 1769480 | tf_op jit(solution)/shard_map/ppermute | solution.py:173
  171.7 16.4 %copy-start.1 = (f32[32,32,384]{2,1,0:T(8,128)S(1)}, f32[32,32,384]{2,1,0:T(8,128)}, u32[]{:S(2)}) copy-start(f32[32,32,384]{2,1,0:T(8,128)} %copy-done) | copy-start | bytes 4718596
  171.7 16.4 %copy-start.3 = (f32[384,384]{0,1:T(8,128)S(1)}, f32[384,384]{0,1:T(8,128)}, u32[]{:S(2)}) copy-start(f32[384,384]{0,1:T(8,128)} %copy.14) | copy-start | bytes 1769476
  171.7 16.4 %copy-start.9 = (f32[128,192]{1,0:T(8,128)S(1)}, f32[128,192]{1,0:T(8,128)}, u32[]{:S(2)}) copy-start(f32[128,192]{1,0:T(8,128)} %mul.135.ax_ref) | copy-start | bytes 294916
  171.7 16.1 %collective-permute-start.22 = (f32[8,48,384]{2,1,0:T(8,128)S(1)}, f32[8,48,384]{2,1,0:T(8,128)S(1)}, u32[]{:S(2)}, u32[]{:S(2)}) collective-permute-start(f32[8,48,384]{2,1,0:T(8,128)S(1)} %get-tuple-element.25), channel_id=1, source_target_pairs={{2,0},{3,1},{4,2},{5,3},{6,4},{7,5},{10,8},{11,9},{12,10},{13,11},... | collective-permute-start | bytes 1769480 | tf_op jit(solution)/shard_map/ppermute | solution.py:173
  196.1 19.7 %collective-permute-start.28 = (f32[8,32,384]{2,1,0:T(8,128)S(1)}, f32[8,32,384]{2,1,0:T(8,128)S(1)}, u32[]{:S(2)}, u32[]{:S(2)}) collective-permute-start(f32[8,32,384]{2,1,0:T(8,128)S(1)} %get-tuple-element.36), channel_id=1, source_target_pairs={{2,0},{3,1},{4,2},{5,3},{6,4},{7,5},{10,8},{11,9},{12,10},{13,11},... | collective-permute-start | bytes 1179656 | tf_op jit(solution)/shard_map/ppermute | solution.py:173
  197.4 18.4 %collective-permute-start.27 = (f32[8,32,384]{2,1,0:T(8,128)S(1)}, f32[8,32,384]{2,1,0:T(8,128)S(1)}, u32[]{:S(2)}, u32[]{:S(2)}) collective-permute-start(f32[8,32,384]{2,1,0:T(8,128)S(1)} %get-tuple-element.37), channel_id=1, source_target_pairs={{0,2},{1,3},{2,4},{3,5},{4,6},{5,7},{8,10},{9,11},{10,12},{11,13},... | collective-permute-start | bytes 1179656 | tf_op jit(solution)/shard_map/ppermute | solution.py:173
  209.8 14.5 %collective-permute-start.24 = (f32[8,32,384]{2,1,0:T(8,128)S(1)}, f32[8,32,384]{2,1,0:T(8,128)S(1)}, u32[]{:S(2)}, u32[]{:S(2)}) collective-permute-start(f32[8,32,384]{2,1,0:T(8,128)S(1)} %get-tuple-element.40), channel_id=1, source_target_pairs={{2,0},{3,1},{4,2},{5,3},{6,4},{7,5},{10,8},{11,9},{12,10},{13,11},... | collective-permute-start | bytes 1179656 | tf_op jit(solution)/shard_map/ppermute | solution.py:173
  211.1 13.2 %collective-permute-start.23 = (f32[8,32,384]{2,1,0:T(8,128)S(1)}, f32[8,32,384]{2,1,0:T(8,128)S(1)}, u32[]{:S(2)}, u32[]{:S(2)}) collective-permute-start(f32[8,32,384]{2,1,0:T(8,128)S(1)} %get-tuple-element.41), channel_id=1, source_target_pairs={{0,2},{1,3},{2,4},{3,5},{4,6},{5,7},{8,10},{9,11},{10,12},{11,13},... | collective-permute-start | bytes 1179656 | tf_op jit(solution)/shard_map/ppermute | solution.py:173
  218.5 14.5 %collective-permute-start.30 = (f32[32,8,384]{2,1,0:T(8,128)S(1)}, f32[32,8,384]{2,1,0:T(8,128)S(1)}, u32[]{:S(2)}, u32[]{:S(2)}) collective-permute-start(f32[32,8,384]{2,1,0:T(8,128)S(1)} %get-tuple-element.34), channel_id=1, source_target_pairs={{1,0},{3,2},{5,4},{7,6},{9,8},{11,10},{13,12},{15,14},{16,17},{17,... | collective-permute-start | bytes 1179656 | tf_op jit(solution)/shard_map/ppermute | solution.py:173
  219.8 13.3 %collective-permute-start.29 = (f32[32,8,384]{2,1,0:T(8,128)S(1)}, f32[32,8,384]{2,1,0:T(8,128)S(1)}, u32[]{:S(2)}, u32[]{:S(2)}) collective-permute-start(f32[32,8,384]{2,1,0:T(8,128)S(1)} %get-tuple-element.35), channel_id=1, source_target_pairs={{0,1},{1,17},{2,3},{3,19},{4,5},{5,21},{6,7},{7,23},{8,9},{9,25},{... | collective-permute-start | bytes 1179656 | tf_op jit(solution)/shard_map/ppermute | solution.py:173
  227.1 6.0 %copy-start.12 = (f32[128,192]{1,0:T(8,128)S(1)}, f32[128,192]{1,0:T(8,128)}, u32[]{:S(2)}) copy-start(f32[128,192]{1,0:T(8,128)} %mul.138.ax_ref) | copy-start | bytes 294916
  227.2 10.5 %collective-permute-start.26 = (f32[32,8,384]{2,1,0:T(8,128)S(1)}, f32[32,8,384]{2,1,0:T(8,128)S(1)}, u32[]{:S(2)}, u32[]{:S(2)}) collective-permute-start(f32[32,8,384]{2,1,0:T(8,128)S(1)} %get-tuple-element.38), channel_id=1, source_target_pairs={{1,0},{3,2},{5,4},{7,6},{9,8},{11,10},{13,12},{15,14},{16,17},{17,... | collective-permute-start | bytes 1179656 | tf_op jit(solution)/shard_map/ppermute | solution.py:173
  228.5 9.8 %collective-permute-start.25 = (f32[32,8,384]{2,1,0:T(8,128)S(1)}, f32[32,8,384]{2,1,0:T(8,128)S(1)}, u32[]{:S(2)}, u32[]{:S(2)}) collective-permute-start(f32[32,8,384]{2,1,0:T(8,128)S(1)} %get-tuple-element.39), channel_id=1, source_target_pairs={{0,1},{1,17},{2,3},{3,19},{4,5},{5,21},{6,7},{7,23},{8,9},{9,25},{... | collective-permute-start | bytes 1179656 | tf_op jit(solution)/shard_map/ppermute | solution.py:173
  242.9 3.6 %collective-permute-start.31 = (f32[32,32,384]{2,1,0:T(8,128)S(1)}, f32[32,32,384]{2,1,0:T(8,128)}, u32[]{:S(2)}, u32[]{:S(2)}) collective-permute-start(f32[32,32,384]{2,1,0:T(8,128)S(1)} %shard_map.57), channel_id=1, source_target_pairs={{0,8},{1,9},{2,10},{3,11},{4,12},{5,13},{6,14},{7,15},{8,0},{9,1},... | collective-permute-start | bytes 4718600 | tf_op jit(solution)/shard_map/ppermute | solution.py:173
  249.3 13.6 %collective-permute-start.34 = (f32[8,32,384]{2,1,0:T(8,128)S(1)}, f32[8,32,384]{2,1,0:T(8,128)S(1)}, u32[]{:S(2)}, u32[]{:S(2)}) collective-permute-start(f32[8,32,384]{2,1,0:T(8,128)S(1)} %get-tuple-element.32), channel_id=1, source_target_pairs={{0,17},{1,16},{2,19},{3,18},{4,21},{5,20},{6,23},{7,22},{8,25},{9,... | collective-permute-start | bytes 1179656 | tf_op jit(solution)/shard_map/ppermute | solution.py:173
  252.8 17.8 %collective-permute-start.32 = (f32[8,32,384]{2,1,0:T(8,128)S(1)}, f32[8,32,384]{2,1,0:T(8,128)S(1)}, u32[]{:S(2)}, u32[]{:S(2)}) collective-permute-start(f32[8,32,384]{2,1,0:T(8,128)S(1)} %get-tuple-element.32), channel_id=1, source_target_pairs={{0,1},{1,0},{2,3},{3,2},{4,5},{5,4},{6,7},{7,6},{8,9},{9,8},{10,11... | collective-permute-start | bytes 1179656 | tf_op jit(solution)/shard_map/ppermute | solution.py:173
  253.4 17.4 %collective-permute-start.33 = (f32[8,32,384]{2,1,0:T(8,128)S(1)}, f32[8,32,384]{2,1,0:T(8,128)S(1)}, u32[]{:S(2)}, u32[]{:S(2)}) collective-permute-start(f32[8,32,384]{2,1,0:T(8,128)S(1)} %get-tuple-element.33), channel_id=1, source_target_pairs={{0,16},{1,17},{2,18},{3,19},{4,20},{5,21},{6,22},{7,23},{8,24},{9,... | collective-permute-start | bytes 1179656 | tf_op jit(solution)/shard_map/ppermute | solution.py:173
  271.2 3.5 %collective-permute-start.35 = (f32[8,128,384]{2,1,0:T(8,128)S(1)}, f32[8,128,384]{2,1,0:T(8,128)S(1)}, u32[]{:S(2)}, u32[]{:S(2)}) collective-permute-start(f32[8,128,384]{2,1,0:T(8,128)S(1)} %pad_maximum_fusion.6), channel_id=1, source_target_pairs={{0,8},{1,9},{2,10},{3,11},{4,12},{5,13},{6,14},{7,15},{8,0},{9,1},... | collective-permute-start | bytes 4718600 | tf_op jit(solution)/shard_map/ppermute | solution.py:173
